TPU v7x, 16 devices: a whole 2x2x2 slice. The times are simulated.
16 devices in a mesh: tp: 2 (over z), dp: 2 (over y), pp: 4 (over x, core).
Axes of the slice: x: 2, y: 2, z: 2, core: 2. Of those that a mesh axis runs over, the one named last changes fastest.
Arguments:
- x_in: bfloat16 [6, 4, 256, 1536], P(None, 'dp', 'tp')
- g_out: bfloat16 [6, 4, 256, 1536], P(None, 'dp', 'tp')
- w_gate: bfloat16 [4, 1, 1536, 6144], P('pp', None, 'dp', 'tp')
- w_in: bfloat16 [4, 1, 1536, 6144], P('pp', None, 'dp', 'tp')
- w_out: bfloat16 [4, 1, 6144, 1536], P('pp', None, 'tp', 'dp')
Outputs:
- output 1: bfloat16 [6, 4, 256, 1536], P(None, 'dp', 'tp')
- output 2: float32 [4, 1, 1536, 6144], P('pp', None, 'dp', 'tp')
- output 3: float32 [4, 1, 1536, 6144], P('pp', None, 'dp', 'tp')
- output 4: float32 [4, 1, 6144, 1536], P('pp', None, 'tp', 'dp')
All inputs are finite; a program needn't handle non-finite values.
Results may differ from a plain program's by a relative error of at most 0.02.
Values are sent between devices in bfloat16 or wider.
A program may use at most 1 GiB of HBM per device.

v0:
```python
import jax
import jax.numpy as jnp
from jax import lax
from jax.experimental import pallas as pl
from jax.experimental.pallas import tpu as pltpu
from jax.sharding import Mesh, PartitionSpec as P

RMS_EPS = 1e-6
CONTRACT_ROWS = (((0,), (0,)), ((), ()))
CONTRACT_COLS = (((1,), (1,)), ((), ()))
ALL_AXES = ('tp', 'dp', 'x', 'core')
COLS = 512
ROWS = 64
ROW_BLOCK = 256
DEPTH = 6
EARLY = 6
RELAYED = 4
VMEM_BYTES = 60 * 1024 * 1024

def rms_parts(h_tok):
    h_f32 = h_tok.astype(jnp.float32)
    inv_rms = lax.rsqrt(jnp.mean(h_f32 * h_f32, axis=-1, keepdims=True) + RMS_EPS)
    return h_f32, inv_rms, (h_f32 * inv_rms).astype(jnp.bfloat16)


def swiglu_parts(normed_all, w_gate_l, w_in_l):
    gate_pre = jnp.dot(normed_all, w_gate_l, preferred_element_type=jnp.float32)
    in_pre = jnp.dot(normed_all, w_in_l, preferred_element_type=jnp.float32)
    gate_sig = jax.nn.sigmoid(gate_pre)
    return gate_pre, in_pre, gate_sig, gate_pre * gate_sig


def stage_place():
    z, y, x, core = (lax.axis_index(name) for name in ALL_AXES)
    after = {'dp': 1 - y, 'x': x + y}
    before = {'dp': 1 - y, 'x': x + y - 1}
    return 2 * x + y, core, {'tp': 1 - z}, after, before


def remote(source, target, send_sem, recv_sem, place):
    return pltpu.make_async_remote_copy(src_ref=source, dst_ref=target, send_sem=send_sem, recv_sem=recv_sem, device_id=place, device_id_type=pl.DeviceIdType.MESH)


def forward_kernel(x_ref, *refs):
    own = refs[:3]
    saved_h, saved_n, x_land = refs[3:6]
    kept = refs[6:9]
    (w_gate, w_in, w_out, h_buf, n_own, n_peer, acc, keep, give, got, h_out,
     w_sem, load_sem, h_send, h_recv, n_send, n_recv, g_send, g_recv, save_h, save_own, save_peer, far_send, far_recv, relay, b_send, b_recv, free) = refs[9:]
    n = x_ref.shape[0]
    rows = x_ref.shape[1]
    hid = w_gate.shape[1]
    stage, core, peer, after, before = stage_place()
    y, x = lax.axis_index('dp'), lax.axis_index('x')
    half = own[0].shape[0]
    direct = hid - hid // RELAYED
    short = stage == 0
    home = core == y

    def mine(k, low, size):
        return own[k].at[pl.ds(low, size), :] if k == 2 else own[k].at[:, pl.ds(low, size)]

    def spot(k, which, low, size):
        part = pl.ds(pl.multiple_of(which * half, half), half)
        return w_out.at[pl.ds(low, size), part] if k == 2 else (w_gate, w_in)[k].at[part, pl.ds(low, size)]

    def local_block(k):
        return pltpu.make_async_copy(mine(k, 0, hid), spot(k, y, 0, hid), w_sem.at[k])

    def block_copy(k, kind, source, target, place):
        return remote(source, target, b_send.at[kind, k], b_recv.at[kind, k], place)

    def partner_block(k):
        return block_copy(k, 0, mine(k, 0, hid), spot(k, y, 0, hid), {'core': 1 - core})

    def away_block(k, size):
        return block_copy(k, 1, mine(k, 0, size), spot(k, y, 0, size), {'dp': 1 - y, 'core': 1 - core})

    def shared_block(k):
        return block_copy(k, 2, spot(k, 1 - y, 0, hid), spot(k, 1 - y, 0, hid), {'core': 1 - core})

    def hop(k, number):
        rest = hid - direct
        source = mine(k, direct, rest) if number == 0 else relay.at[k]
        target = spot(k, 1, direct, rest) if number == 2 else relay.at[k]
        place = ({'x': 1, 'core': 1}, {'dp': 0, 'core': 0}, {'x': 0, 'core': 1})[number]
        return block_copy(k, 3, source, target, place)

    hop_from = ((stage == 1) & (core == 0), (stage == 3) & (core == 1), (stage == 2) & (core == 0))

    @pl.when(home)
    def _():
        for k in range(3):
            partner_block(k).start()
            local_block(k).start()

    @pl.when(jnp.logical_not(home) & (stage == 1))
    def _():
        for k in range(3):
            hop(k, 0).start()
            away_block(k, direct).start()

    @pl.when(jnp.logical_not(home) & (stage != 1))
    def _():
        for k in range(3):
            away_block(k, hid).start()

    for number in (1, 2):
        @pl.when(hop_from[number])
        def _(number=number):
            for k in range(3):
                hop(k, number - 1).wait_recv()
                hop(k, number).start()

    def weights_ready():
        @pl.when(home)
        def _():
            for k in range(3):
                local_block(k).wait()
                shared_block(k).wait_recv()

        @pl.when(jnp.logical_not(home))
        def _():
            for k in range(3):
                @pl.when(short)
                def _():
                    away_block(k, direct).wait_recv()
                    hop(k, 2).wait_recv()

                @pl.when(jnp.logical_not(short))
                def _():
                    away_block(k, hid).wait_recv()

                shared_block(k).start()
            for k in range(3):
                partner_block(k).wait_recv()

        for k in range(3):
            keep_weight(k).start()

    def keep_weight(k):
        return pltpu.make_async_copy((w_gate, w_in, w_out)[k], kept[k], w_sem.at[3 + k])

    def push(low, high):
        @pl.when((stage == 1) & (core == 1))
        def _():
            @pl.loop(low, high)
            def _(c):
                far_copy(c).start()

    def x_load(c, source):
        return pltpu.make_async_copy(source.at[c], h_buf.at[lax.rem(c, DEPTH)], load_sem.at[lax.rem(c, 2)])

    def far_copy(c):
        return remote(x_ref.at[c], x_land.at[c], far_send.at[c], far_recv.at[c], {'dp': 0})

    def start_load(c):
        @pl.when(core == 0)
        def _():
            x_load(c, x_ref).start()

        @pl.when(core == 1)
        def _():
            far_copy(c).wait_recv()
            x_load(c, x_land).start()

    push(0, EARLY)

    @pl.when(stage > 0)
    def _():
        weights_ready()

    def h_copy(c):
        return remote(h_out.at[lax.rem(c, 2)], h_buf.at[lax.rem(c, DEPTH)], h_send.at[lax.rem(c, 2)], h_recv.at[lax.rem(c, DEPTH)], after)

    def n_copy(c):
        s = lax.rem(c, 4)
        return remote(n_own.at[s], n_peer.at[s], n_send.at[s], n_recv.at[s], peer)

    def give_copy(c):
        s = lax.rem(c, 3)
        return remote(give.at[s], got.at[s], g_send.at[s], g_recv.at[s], peer)

    def keep_h(c):
        s = lax.rem(c, DEPTH)
        return pltpu.make_async_copy(h_buf.at[s], saved_h.at[c], save_h.at[s])

    def keep_own(c):
        s = lax.rem(c, 4)
        return pltpu.make_async_copy(n_own.at[s], saved_n.at[c, pl.ds(0, rows)], save_own.at[s])

    def keep_peer(c):
        s = lax.rem(c, 4)
        return pltpu.make_async_copy(n_peer.at[s], saved_n.at[c, pl.ds(rows, rows)], save_peer.at[s])

    @pl.when(stage == 0)
    def _():
        start_load(0)

    def body(i, carry):
        @pl.when(i < n)
        def _():
            @pl.when(stage == 0)
            def _():
                x_load(i, x_ref).wait()

                @pl.when(i + 1 < n)
                def _():
                    start_load(i + 1)

            @pl.when(stage > 0)
            def _():
                h_copy(i).wait_recv()

            keep_h(i).start()

            @pl.when(i >= 4)
            def _():
                n_copy(i - 4).wait_send()
                keep_own(i - 4).wait()

            n_own[lax.rem(i, 4)] = rms_parts(h_buf[lax.rem(i, DEPTH)])[2]
            n_copy(i).start()
            keep_own(i).start()

        @pl.when(i == 0)
        def _():
            push(EARLY, n)

        @pl.when((i == 1) & (stage == 0))
        def _():
            weights_ready()

        @pl.when((i >= 1) & (i <= n))
        def _():
            c = i - 1
            s = lax.rem(c, 3)
            n_copy(c).wait_recv()
            keep_peer(c).start()
            @pl.when(stage < 3)
            def _():
                both = jnp.concatenate([n_own[lax.rem(c, 4)], n_peer[lax.rem(c, 4)]], 0)
                for j in range(hid // COLS):
                    part = pl.ds(j * COLS, COLS)
                    gate_pre, in_pre, gate_sig, gate_act = swiglu_parts(both, w_gate[:, part], w_in[:, part])
                    branch = jnp.dot((gate_act * in_pre).astype(jnp.bfloat16), w_out[part, :], preferred_element_type=jnp.float32)
                    acc[...] = branch if j == 0 else acc[...] + branch
                keep[s] = acc[:rows]
                give[s] = acc[rows:]

            keep_peer(c).wait()

            @pl.when(stage < 3)
            def _():
                give_copy(c).start()

        @pl.when(i >= 2)
        def _():
            c = i - 2
            s = lax.rem(c, 3)
            keep_h(c).wait()

            @pl.when(stage < 3)
            def _():
                give_copy(c).wait_recv()
                give_copy(c).wait_send()

                @pl.when(c >= 2)
                def _():
                    h_copy(c - 2).wait_send()

                h_out[lax.rem(c, 2)] = h_buf[lax.rem(c, DEPTH)] + (keep[s] + got[s]).astype(jnp.bfloat16)

                @pl.when(c >= DEPTH)
                def _():
                    pl.semaphore_wait(free, 1)

                h_copy(c).start()

            @pl.when((stage > 0) & (c < n - DEPTH))
            def _():
                pl.semaphore_signal(free, inc=1, device_id=before, device_id_type=pl.DeviceIdType.MESH)

        return carry

    lax.fori_loop(0, n + 2, body, 0)
    for c in range(n - 4, n):
        n_copy(c).wait_send()
        keep_own(c).wait()

    @pl.when((stage == 1) & (core == 1))
    def _():
        @pl.loop(0, n)
        def _(c):
            far_copy(c).wait_send()

    for number in range(3):
        @pl.when(hop_from[number])
        def _(number=number):
            for k in range(3):
                hop(k, number).wait_send()

    for k in range(3):
        keep_weight(k).wait()

        @pl.when(home)
        def _():
            partner_block(k).wait_send()

        @pl.when(jnp.logical_not(home))
        def _():
            shared_block(k).wait_send()

            @pl.when(stage == 1)
            def _():
                away_block(k, direct).wait_send()

            @pl.when(stage != 1)
            def _():
                away_block(k, hid).wait_send()

    @pl.when(stage < 3)
    def _():
        for c in range(n - 2, n):
            h_copy(c).wait_send()


def backward_kernel(g_ref, saved_h, saved_n, *refs):
    kept = refs[:3]
    dx_ref, saved_e, saved_u, saved_da, saved_db, g_land = refs[3:9]
    (w_gate, w_in, w_out, e_buf, e_peer, n_buf, h_buf, acc, keep, give, got, e_out, u_out, da_out, db_out,
     w_sem, load_sem, n_sem, h_sem, s_send, s_recv, e_send, e_recv, g_send, g_recv, save_own, save_peer, save_u, save_da, save_db, dx_sem, dx_send, dx_recv, far_send, far_recv, free) = refs[9:]
    n = g_ref.shape[0]
    rows = g_ref.shape[1]
    hid = w_gate.shape[1]
    stage, core, peer, after, before = stage_place()
    loads = [pltpu.make_async_copy(kept[k], (w_gate, w_in, w_out)[k], w_sem.at[k]) for k in range(3)]
    for load in loads:
        load.start()

    def g_load(c, source):
        return pltpu.make_async_copy(source.at[c], e_buf.at[lax.rem(c, DEPTH)], load_sem.at[lax.rem(c, 2)])

    def far_copy(c):
        return remote(g_ref.at[c], g_land.at[c], far_send.at[c], far_recv.at[c], {'dp': 1})

    def start_load(c):
        @pl.when(core == 1)
        def _():
            g_load(c, g_ref).start()

        @pl.when(core == 0)
        def _():
            far_copy(c).wait_recv()
            g_load(c, g_land).start()

    @pl.when((stage == 2) & (core == 0))
    def _():
        @pl.loop(0, n)
        def _(c):
            far_copy(c).start()

    def n_load(c):
        s = lax.rem(c, 3)
        return pltpu.make_async_copy(saved_n.at[c], n_buf.at[s], n_sem.at[s])

    def h_load(c):
        s = lax.rem(c, 3)
        return pltpu.make_async_copy(saved_h.at[c], h_buf.at[s], h_sem.at[s])

    def stage_copy(c):
        return remote(e_out.at[lax.rem(c, 2)], e_buf.at[lax.rem(c, DEPTH)], s_send.at[lax.rem(c, 2)], s_recv.at[lax.rem(c, DEPTH)], before)

    def e_copy(c):
        s = lax.rem(c, 3)
        return remote(e_buf.at[lax.rem(c, DEPTH)], e_peer.at[s], e_send.at[s], e_recv.at[s], peer)

    def give_copy(c):
        s = lax.rem(c, 3)
        return remote(give.at[s], got.at[s], g_send.at[s], g_recv.at[s], peer)

    def keep_own(c):
        return pltpu.make_async_copy(e_buf.at[lax.rem(c, DEPTH)], saved_e.at[c, pl.ds(0, rows)], save_own.at[lax.rem(c, 3)])

    def keep_peer(c):
        s = lax.rem(c, 3)
        return pltpu.make_async_copy(e_peer.at[s], saved_e.at[c, pl.ds(rows, rows)], save_peer.at[s])

    def keep_wide(c):
        s = lax.rem(c, 2)
        return [pltpu.make_async_copy(source.at[s], target.at[c], sem.at[s])
                for source, target, sem in ((u_out, saved_u, save_u), (da_out, saved_da, save_da), (db_out, saved_db, save_db))]

    def keep_dx(c):
        s = lax.rem(c, 2)
        return pltpu.make_async_copy(e_out.at[s], dx_ref.at[c], dx_sem.at[s])

    def dx_copy(c, k):
        s = lax.rem(c, 2)
        return remote(e_out.at[s], dx_ref.at[c], dx_send.at[s, k], dx_recv.at[0], {'dp': core, 'x': k // 2, 'core': k % 2})

    def dx_start(c):
        @pl.when(core == 0)
        def _():
            keep_dx(c).start()

        @pl.when(core == 1)
        def _():
            dx_copy(c, 0).start()

        for k in range(1, 4):
            dx_copy(c, k).start()

    def dx_done(c):
        @pl.when(core == 0)
        def _():
            keep_dx(c).wait()

        @pl.when(core == 1)
        def _():
            dx_copy(c, 0).wait_send()

        for k in range(1, 4):
            dx_copy(c, k).wait_send()

    @pl.when(stage == 3)
    def _():
        start_load(0)

    def body(i, carry):
        @pl.when(i < n)
        def _():
            n_load(i).start()
            h_load(i).start()

            @pl.when(stage == 3)
            def _():
                g_load(i, g_ref).wait()

                @pl.when(i + 1 < n)
                def _():
                    start_load(i + 1)

            @pl.when(stage < 3)
            def _():
                stage_copy(i).wait_recv()

            e_copy(i).start()
            keep_own(i).start()

        @pl.when(i == 1)
        def _():
            for load in loads:
                load.wait()

        @pl.when((i >= 1) & (i <= n))
        def _():
            c = i - 1
            s = lax.rem(c, 3)
            w = lax.rem(c, 2)
            n_load(c).wait()
            e_copy(c).wait_recv()
            keep_peer(c).start()

            @pl.when(c >= 2)
            def _():
                for copy in keep_wide(c - 2):
                    copy.wait()

            normed = n_buf[s]
            both = jnp.concatenate([e_buf[lax.rem(c, DEPTH)], e_peer[s]], 0)
            for j in range(hid // COLS):
                part = pl.ds(j * COLS, COLS)
                gate_pre, in_pre, gate_sig, gate_act = swiglu_parts(normed, w_gate[:, part], w_in[:, part])
                d_hidden = lax.dot_general(both, w_out[part, :], CONTRACT_COLS, preferred_element_type=jnp.float32).astype(jnp.bfloat16).astype(jnp.float32)
                u_out[w, :, part] = (gate_act * in_pre).astype(jnp.bfloat16)
                d_gate = (d_hidden * in_pre * (gate_sig * (1.0 + gate_pre * (1.0 - gate_sig)))).astype(jnp.bfloat16)
                d_up = (d_hidden * gate_act).astype(jnp.bfloat16)
                da_out[w, :, part] = d_gate
                db_out[w, :, part] = d_up
            for copy in keep_wide(c):
                copy.start()
            acc[...] = lax.dot_general(da_out[w], w_gate[...], CONTRACT_COLS, preferred_element_type=jnp.float32) + lax.dot_general(db_out[w], w_in[...], CONTRACT_COLS, preferred_element_type=jnp.float32)
            keep[s] = acc[:rows]
            give[s] = acc[rows:]
            keep_peer(c).wait()
            give_copy(c).start()

        @pl.when(i >= 2)
        def _():
            c = i - 2
            s = lax.rem(c, 3)
            w = lax.rem(c, 2)
            h_load(c).wait()
            give_copy(c).wait_recv()
            give_copy(c).wait_send()
            e_copy(c).wait_send()
            keep_own(c).wait()

            @pl.when(c >= 2)
            def _():
                @pl.when(stage > 0)
                def _():
                    stage_copy(c - 2).wait_send()

                @pl.when(stage == 0)
                def _():
                    dx_done(c - 2)

            d_norm = keep[s] + got[s]
            h_f32, inv_rms, _ = rms_parts(h_buf[s])
            unit_rms = h_f32 * inv_rms
            d_h = inv_rms * (d_norm - unit_rms * jnp.mean(d_norm * unit_rms, axis=-1, keepdims=True))
            e_out[w] = (e_buf[lax.rem(c, DEPTH)].astype(jnp.float32) + d_h).astype(jnp.bfloat16)

            @pl.when(stage > 0)
            def _():
                @pl.when(c >= DEPTH)
                def _():
                    pl.semaphore_wait(free, 1)

                stage_copy(c).start()

            @pl.when(stage == 0)
            def _():
                dx_start(c)

            @pl.when((stage < 3) & (c < n - DEPTH))
            def _():
                pl.semaphore_signal(free, inc=1, device_id=after, device_id_type=pl.DeviceIdType.MESH)

        return carry

    lax.fori_loop(0, n + 2, body, 0)
    for c in range(n - 2, n):
        for copy in keep_wide(c):
            copy.wait()

        @pl.when(stage > 0)
        def _():
            stage_copy(c).wait_send()

        @pl.when(stage == 0)
        def _():
            dx_done(c)

    @pl.when((stage > 0) | (core > 0))
    def _():
        remote(dx_ref, dx_ref, dx_send.at[0, 0], dx_recv.at[0], peer).wait_recv()

    @pl.when((stage == 2) & (core == 0))
    def _():
        @pl.loop(0, n)
        def _(c):
            far_copy(c).wait_send()


def common_scratch(width, hid, rows):
    return [pltpu.VMEM((width, hid), jnp.bfloat16), pltpu.VMEM((width, hid), jnp.bfloat16), pltpu.VMEM((hid, width), jnp.bfloat16),
            pltpu.VMEM((DEPTH, rows, width), jnp.bfloat16)]


def partial_scratch(width, rows):
    return [pltpu.VMEM((2 * rows, width), jnp.float32)] + [pltpu.VMEM((3, rows, width), jnp.float32)] * 3 + [pltpu.VMEM((2, rows, width), jnp.bfloat16)]


def dma(*sizes):
    return [pltpu.SemaphoreType.DMA((size,)) for size in sizes]


def forward_phase(x_chunks, blocks):
    n, rows, width = x_chunks.shape
    half, hid = blocks[0].shape
    whole = [jax.ShapeDtypeStruct((width, hid), jnp.bfloat16)] * 2 + [jax.ShapeDtypeStruct((hid, width), jnp.bfloat16)]
    anywhere = pl.BlockSpec(memory_space=pl.ANY)
    return pl.pallas_call(
        forward_kernel,
        in_specs=[anywhere] * 4,
        out_specs=[anywhere] * 6,
        out_shape=[jax.ShapeDtypeStruct((n, rows, width), jnp.bfloat16), jax.ShapeDtypeStruct((n, 2 * rows, width), jnp.bfloat16), jax.ShapeDtypeStruct((n, rows, width), jnp.bfloat16)] + whole,
        scratch_shapes=common_scratch(width, hid, rows) + [pltpu.VMEM((4, rows, width), jnp.bfloat16)] * 2 + partial_scratch(width, rows)
        + dma(6, 2, 2, DEPTH, 4, 4, 3, 3, DEPTH, 4, 4, n, n)
        + [pltpu.VMEM((3, half, hid // RELAYED), jnp.bfloat16), pltpu.SemaphoreType.DMA((4, 3)), pltpu.SemaphoreType.DMA((4, 3))] + [pltpu.SemaphoreType.REGULAR],
        cost_estimate=pl.CostEstimate(flops=12 * n * rows * width * hid, bytes_accessed=6 * width * hid, transcendentals=0),
        compiler_params=pltpu.CompilerParams(has_side_effects=True, vmem_limit_bytes=VMEM_BYTES),
        name="forward_phase",
    )(x_chunks, *blocks)


def backward_phase(g_chunks, saved_h, saved_n, blocks):
    n, rows, width = g_chunks.shape
    hid = blocks[0].shape[1]
    anywhere = pl.BlockSpec(memory_space=pl.ANY)
    wide = jax.ShapeDtypeStruct((n, 2 * rows, hid), jnp.bfloat16)
    return pl.pallas_call(
        backward_kernel,
        in_specs=[anywhere] * 6,
        out_specs=[anywhere] * 6,
        out_shape=[jax.ShapeDtypeStruct((n, rows, width), jnp.bfloat16), jax.ShapeDtypeStruct((n, 2 * rows, width), jnp.bfloat16), wide, wide, wide, jax.ShapeDtypeStruct((n, rows, width), jnp.bfloat16)],
        scratch_shapes=common_scratch(width, hid, rows)
        + [pltpu.VMEM((3, rows, width), jnp.bfloat16), pltpu.VMEM((3, 2 * rows, width), jnp.bfloat16), pltpu.VMEM((3, rows, width), jnp.bfloat16)]
        + partial_scratch(width, rows) + [pltpu.VMEM((2, 2 * rows, hid), jnp.bfloat16)] * 3
        + dma(3, 2, 3, 3, 2, DEPTH, 3, 3, 3, 3, 3, 3, 2, 2, 2, 2) + [pltpu.SemaphoreType.DMA((2, 4))] + dma(1, n, n) + [pltpu.SemaphoreType.REGULAR],
        cost_estimate=pl.CostEstimate(flops=20 * n * rows * width * hid, bytes_accessed=6 * width * hid, transcendentals=0),
        compiler_params=pltpu.CompilerParams(has_side_effects=True, vmem_limit_bytes=VMEM_BYTES),
        name="backward_phase",
    )(g_chunks, saved_h, saved_n, *blocks)


def gradient_kernel(n_ref, e_ref, da_ref, db_ref, u_ref, dw_gate, dw_in, dw_out,
                    raw, flipped, tile, mine, give, got, total, total_t,
                    raw_sem, tile_sem, p_send, p_recv, keep_sem, keep_t_sem, far_send, far_t_send, far_recv):
    z, y, x, core = (lax.axis_index(name) for name in ALL_AXES)
    tokens, width = n_ref.shape
    hid = da_ref.shape[1]
    half = width // 2
    tiles = hid // COLS
    steps = tokens // COLS
    home = core == y
    swap = {'dp': 1 - y, 'core': 1 - core}
    sources = (da_ref, db_ref, u_ref)
    targets = (dw_gate, dw_in, dw_out)

    def cols(j):
        return pl.ds(pl.multiple_of(j * COLS, COLS), COLS)

    def raw_load(source, k):
        return pltpu.make_async_copy(source.at[cols(k)], raw.at[lax.rem(k, 2)], raw_sem.at[lax.rem(k, 2)])

    def tile_load(a, j):
        s = lax.rem(a * tiles + j, 2)
        return pltpu.make_async_copy(sources[a].at[:, cols(j)], tile.at[s], tile_sem.at[s])

    def part_copy(t):
        s = lax.rem(t, 2)
        return remote(give.at[s], got.at[s], p_send.at[s], p_recv.at[s], {'core': 1 - core})

    def place(a, j):
        return (total_t if a == 2 else total).at[lax.rem(j, 3)], (targets[a].at[cols(j)] if a == 2 else targets[a].at[:, cols(j)])

    def home_copy(a, j):
        source, target = place(a, j)
        return pltpu.make_async_copy(source, target, (keep_t_sem if a == 2 else keep_sem).at[lax.rem(j, 3)])

    def far_copy(a, j):
        source, target = place(a, j)
        return remote(source, target, (far_t_send if a == 2 else far_send).at[lax.rem(j, 3)], far_recv.at[a], swap)

    def shipped(a, j):
        @pl.when(home)
        def _():
            home_copy(a, j).wait()

        @pl.when(jnp.logical_not(home))
        def _():
            far_copy(a, j).wait_send()

    def flip(source):
        raw_load(source, 0).start()

        @pl.loop(0, steps)
        def _(k):
            raw_load(source, k).wait()

            @pl.when(k + 1 < steps)
            def _():
                raw_load(source, k + 1).start()

            flipped[:, cols(k)] = raw[lax.rem(k, 2)].T

    tile_load(0, 0).start()
    for a in range(3):
        if a != 1:
            flip(n_ref if a == 0 else e_ref)

        @pl.loop(0, tiles)
        def _(j, a=a):
            t = a * tiles + j
            s = lax.rem(t, 2)
            tile_load(a, j).wait()

            @pl.when(j + 1 < tiles)
            def _():
                tile_load(a, j + 1).start()

            if a < 2:
                @pl.when(j + 1 == tiles)
                def _():
                    tile_load(a + 1, 0).start()

            @pl.when(t >= 2)
            def _():
                part_copy(t - 2).wait_send()

            @pl.loop(0, half // ROW_BLOCK)
            def _(m):
                part = pl.ds(pl.multiple_of(m * ROW_BLOCK, ROW_BLOCK), ROW_BLOCK)
                theirs = pl.ds(pl.multiple_of((1 - core) * half + m * ROW_BLOCK, ROW_BLOCK), ROW_BLOCK)
                give[s, part] = jnp.dot(flipped[theirs, :], tile[s], preferred_element_type=jnp.float32)

            part_copy(t).start()

            @pl.loop(0, half // ROW_BLOCK)
            def _(m):
                part = pl.ds(pl.multiple_of(m * ROW_BLOCK, ROW_BLOCK), ROW_BLOCK)
                ours = pl.ds(pl.multiple_of(core * half + m * ROW_BLOCK, ROW_BLOCK), ROW_BLOCK)
                mine[part] = jnp.dot(flipped[ours, :], tile[s], preferred_element_type=jnp.float32)

            @pl.when(j >= 3)
            def _():
                shipped(a, j - 3)

            if a == 1:
                @pl.when(j < 3)
                def _():
                    shipped(0, tiles - 3 + j)

            part_copy(t).wait_recv()
            w = lax.rem(j, 3)
            if a == 2:
                total_t[w] = (mine[...] + got[s]).T
            else:
                total[w] = mine[...] + got[s]

            @pl.when(home)
            def _():
                home_copy(a, j).start()

            @pl.when(jnp.logical_not(home))
            def _():
                far_copy(a, j).start()

    for a in (1, 2):
        for j in range(tiles - 3, tiles):
            shipped(a, j)
    for t in range(3 * tiles - 2, 3 * tiles):
        part_copy(t).wait_send()

    @pl.when(jnp.logical_not(home))
    def _():
        for a in range(3):
            remote(targets[a], targets[a], far_send.at[0], far_recv.at[a], swap).wait_recv()


def gradients(n_flat, e_flat, da_flat, db_flat, u_flat):
    tokens, width = n_flat.shape
    hid = da_flat.shape[1]
    half = width // 2
    anywhere = pl.BlockSpec(memory_space=pl.ANY)
    return pl.pallas_call(
        gradient_kernel,
        in_specs=[anywhere] * 5,
        out_specs=[anywhere] * 3,
        out_shape=[jax.ShapeDtypeStruct((half, hid), jnp.float32)] * 2 + [jax.ShapeDtypeStruct((hid, half), jnp.float32)],
        scratch_shapes=[pltpu.VMEM((2, COLS, width), jnp.bfloat16), pltpu.VMEM((width, tokens), jnp.bfloat16), pltpu.VMEM((2, tokens, COLS), jnp.bfloat16),
                        pltpu.VMEM((half, COLS), jnp.float32), pltpu.VMEM((2, half, COLS), jnp.float32), pltpu.VMEM((2, half, COLS), jnp.float32),
                        pltpu.VMEM((3, half, COLS), jnp.float32), pltpu.VMEM((3, COLS, half), jnp.float32)]
        + dma(2, 2, 2, 2, 3, 3, 3, 3, 3),
        cost_estimate=pl.CostEstimate(flops=6 * tokens * width * hid, bytes_accessed=6 * tokens * hid, transcendentals=0),
        compiler_params=pltpu.CompilerParams(has_side_effects=True, vmem_limit_bytes=VMEM_BYTES),
        name="gradients",
    )(n_flat, e_flat, da_flat, db_flat, u_flat)


def solution(mesh):
    fine = Mesh(mesh.devices.reshape(2, 2, 2, 2), ALL_AXES)
    act_spec = P(None, 'dp', 'tp', None)
    up_spec = P(('x', 'core'), None, 'dp', 'tp')
    down_spec = P(('x', 'core'), None, 'tp', 'dp')

    def train_step(x_in, g_out, w_gate, w_in, w_out):
        width = x_in.shape[3]
        x_in_chunks = x_in.reshape(-1, ROWS, width)
        g_in_chunks = g_out.reshape(-1, ROWS, width)
        n_chunks = x_in_chunks.shape[0]

        saved_h, saved_n, _, *weights = forward_phase(x_in_chunks, [w[0, 0] for w in (w_gate, w_in, w_out)])
        dx, saved_e, saved_u, saved_da, saved_db, _ = backward_phase(g_in_chunks, saved_h, saved_n, weights)

        def flat(array):
            return array.reshape(n_chunks * 2 * ROWS, array.shape[-1])

        grads = gradients(flat(saved_n), flat(saved_e), flat(saved_da), flat(saved_db), flat(saved_u))
        dw_gate, dw_in, dw_out = (grad[None, None] for grad in grads)
        return dx.reshape(x_in.shape), dw_gate, dw_in, dw_out

    return jax.shard_map(train_step, mesh=fine, in_specs=(act_spec, act_spec, up_spec, up_spec, down_spec), out_specs=(act_spec, up_spec, up_spec, down_spec), check_vma=False)
```

profile of v0, /device:TPU:1, one launch (start us, length us, event | category | flops | bytes accessed | tf_op | source)
XLA Modules:
  0.0 1346.1 jit_solution(1791293661248745047)
XLA Ops:
  0.6 436.0 %forward_phase.1 = (bf16[24,64,1536]{2,1,0:T(8,128)(2,1)}, bf16[24,128,1536]{2,1,0:T(8,128)(2,1)}, bf16[24,64,1536]{2,1,0:T(8,128)(2,1)}, bf16[1536,3072]{1,0:T(...) custom-call(bf16[24,64,1536]{2,1,0:T(8,128)(2,1)} %bitcast.20, bf16[768,3072]{1,0:T(8,128)(2,1)} %bitcast.21, ...), custom_call_target="tpu_custom_call" | custom-call | flops 86973087744 | bytes 28311552 | tf_op jit(solution)/shard_map/forward_phase/pallas_call | solution.py:576
  436.6 554.9 %backward_phase.1 = (bf16[24,64,1536]{2,1,0:T(8,128)(2,1)}, bf16[24,128,1536]{2,1,0:T(8,128)(2,1)}, bf16[24,128,3072]{2,1,0:T(8,128)(2,1)}, bf16[24,128,3072]{2,...) custom-call(bf16[24,64,1536]{2,1,0:T(8,128)(2,1)} %bitcast.24, ...), custom_call_target="tpu_custom_call" | custom-call | flops 144955146240 | bytes 28311552 | tf_op jit(solution)/shard_map/backward_phase/pallas_call | solution.py:595
  991.5 330.0 %gradients.1 = (f32[768,3072]{1,0:T(8,128)}, f32[768,3072]{1,0:T(8,128)}, f32[3072,768]{1,0:T(8,128)}) custom-call(bf16[3072,1536]{1,0:T(8,128)(2,1)} %bitcast.28, bf16[3072,1536]{1,0:T(8,128)(2,1)} %bitcast.29, bf16[3072,3072]{1,0:T(8,128)(2,1)} %bitcast.26, bf16[3072,3072]{1,0:T(8,128)(2,1)} %bitcast.27, bf16[3072,3072]{1,0:T(8,128)(2,1)} %bitcast.25), custom_call_target="tpu_custom_call" | custom-call | flops 86973087744 | bytes 56623104 | tf_op jit(solution)/shard_map/gradients/pallas_call | solution.py:750
  1321.5 4.8 copy.13
  1326.4 0.0 copy-start
  1326.4 0.0 slice-start
  1326.4 0.0 slice-start.1
  1326.4 9.8 copy.14
  1336.2 0.0 copy-done
  1336.2 0.0 slice-start.2
  1336.2 4.8 copy.15
  1341.0 0.0 slice-done
  1341.0 0.9 slice-done.1
  1341.9 0.5 slice-done.2
  1342.4 3.7 copy.16
  (1 shorter events, 0.0 us)
Async XLA Ops:
  1326.4 9.8 copy-start
  1326.4 14.6 %slice-start = ((s8[9437184]{0:T(1024)(128)(4,1)}), s8[4194304]{0:T(1024)(128)(4,1)S(1)}, s32[]{:S(2)}) async-start(s8[9437184]{0:T(1024)(128)(4,1)} %bitcast.14), calls=%async_computation | async-start | bytes 8388608
  1326.4 15.5 %slice-start.1 = ((s8[9437184]{0:T(1024)(128)(4,1)}), s8[4194304]{0:T(1024)(128)(4,1)S(1)}, s32[]{:S(2)}) async-start(s8[9437184]{0:T(1024)(128)(4,1)} %bitcast.14), calls=%async_computation.1 | async-start | bytes 8388608
  1336.2 6.2 slice-start.2
where the time goes:
time: 1350 us
  Pallas kernels  1320 us (98%)
  local copies, waits for them, and re-layouts  24.6 us (2%)
    pallas_call x1, Pallas kernels, backward_phase(): pl.pallas_call(backward_kernel, in_specs=[anywhere] * 6, out_specs=[anywh...  555 us
    pallas_call x1, Pallas kernels, forward_phase(): pl.pallas_call(forward_kernel, in_specs=[anywhere] * 4, out_specs=[anywhe...  436 us
    pallas_call x1, Pallas kernels, gradients(): pl.pallas_call(gradient_kernel, in_specs=[anywhere] * 5, out_specs=[anywh...  330 us

commit v1 on v0

--- a/solution.py
+++ b/solution.py
@@ -45,8 +45,9 @@
     own = refs[:3]
     saved_h, saved_n, x_land = refs[3:6]
     kept = refs[6:9]
+    kept_t = refs[9]
     (w_gate, w_in, w_out, h_buf, n_own, n_peer, acc, keep, give, got, h_out,
-     w_sem, load_sem, h_send, h_recv, n_send, n_recv, g_send, g_recv, save_h, save_own, save_peer, far_send, far_recv, relay, b_send, b_recv, free) = refs[9:]
+     w_sem, load_sem, h_send, h_recv, n_send, n_recv, g_send, g_recv, save_h, save_own, save_peer, far_send, far_recv, relay, flipped, b_send, b_recv, free) = refs[10:]
     n = x_ref.shape[0]
     rows = x_ref.shape[1]
     hid = w_gate.shape[1]
@@ -170,6 +171,17 @@
     def _():
         weights_ready()
 
+    keep_flipped = pltpu.make_async_copy(flipped, kept_t, w_sem.at[6])
+
+    @pl.when(stage == 3)
+    def _():
+        @pl.loop(0, hid // COLS)
+        def _(k):
+            part = pl.ds(pl.multiple_of(k * COLS, COLS), COLS)
+            flipped[:, part] = w_out[part, :].T
+
+        keep_flipped.start()
+
     def h_copy(c):
         return remote(h_out.at[lax.rem(c, 2)], h_buf.at[lax.rem(c, DEPTH)], h_send.at[lax.rem(c, 2)], h_recv.at[lax.rem(c, DEPTH)], after)
 
@@ -300,6 +312,10 @@
             for k in range(3):
                 hop(k, number).wait_send()
 
+    @pl.when(stage == 3)
+    def _():
+        keep_flipped.wait()
+
     for k in range(3):
         keep_weight(k).wait()
 
@@ -327,16 +343,67 @@
 
 def backward_kernel(g_ref, saved_h, saved_n, *refs):
     kept = refs[:3]
-    dx_ref, saved_e, saved_u, saved_da, saved_db, g_land = refs[3:9]
+    kept_t = refs[3]
+    dx_ref, saved_e, saved_u, saved_da, saved_db, g_land, n_t = refs[4:11]
     (w_gate, w_in, w_out, e_buf, e_peer, n_buf, h_buf, acc, keep, give, got, e_out, u_out, da_out, db_out,
-     w_sem, load_sem, n_sem, h_sem, s_send, s_recv, e_send, e_recv, g_send, g_recv, save_own, save_peer, save_u, save_da, save_db, dx_sem, dx_send, dx_recv, far_send, far_recv, free) = refs[9:]
+     w_sem, load_sem, n_sem, h_sem, s_send, s_recv, e_send, e_recv, g_send, g_recv, save_own, save_peer, save_u, save_da, save_db, dx_sem, dx_send, dx_recv, far_send, far_recv, raw_w, raw_n, turned, flip_sem, turn_sem, free) = refs[11:]
     n = g_ref.shape[0]
     rows = g_ref.shape[1]
     hid = w_gate.shape[1]
     stage, core, peer, after, before = stage_place()
-    loads = [pltpu.make_async_copy(kept[k], (w_gate, w_in, w_out)[k], w_sem.at[k]) for k in range(3)]
+    loads = [pltpu.make_async_copy(kept[k], (w_gate, w_in)[k], w_sem.at[k]) for k in range(2)]
+    load_out = pltpu.make_async_copy(kept_t, w_out, w_sem.at[2])
     for load in loads:
         load.start()
+
+    def cols(k):
+        return pl.ds(pl.multiple_of(k * COLS, COLS), COLS)
+
+    def flip_weight():
+        def raw_load(k):
+            return pltpu.make_async_copy(kept[2].at[cols(k)], raw_w.at[lax.rem(k, 2)], flip_sem.at[lax.rem(k, 2)])
+
+        raw_load(0).start()
+
+        @pl.loop(0, hid // COLS)
+        def _(k):
+            raw_load(k).wait()
+
+            @pl.when(k + 1 < hid // COLS)
+            def _():
+                raw_load(k + 1).start()
+
+            w_out[:, cols(k)] = raw_w[lax.rem(k, 2)].T
+
+    def flip_normed():
+        each = COLS // (2 * rows)
+        steps = n // each
+
+        def raw_load(k):
+            return pltpu.make_async_copy(saved_n.at[pl.ds(k * each, each)], raw_n.at[lax.rem(k, 2)], flip_sem.at[lax.rem(k, 2)])
+
+        def store(k):
+            return pltpu.make_async_copy(turned.at[lax.rem(k, 2)], n_t.at[:, cols(k)], turn_sem.at[lax.rem(k, 2)])
+
+        raw_load(0).start()
+
+        @pl.loop(0, steps)
+        def _(k):
+            raw_load(k).wait()
+
+            @pl.when(k + 1 < steps)
+            def _():
+                raw_load(k + 1).start()
+
+            @pl.when(k >= 2)
+            def _():
+                store(k - 2).wait()
+
+            turned[lax.rem(k, 2)] = raw_n[lax.rem(k, 2)].reshape(COLS, raw_n.shape[-1]).T
+            store(k).start()
+
+        for k in range(steps - 2, steps):
+            store(k).wait()
 
     def g_load(c, source):
         return pltpu.make_async_copy(source.at[c], e_buf.at[lax.rem(c, DEPTH)], load_sem.at[lax.rem(c, 2)])
@@ -425,7 +492,13 @@
 
     @pl.when(stage == 3)
     def _():
+        load_out.start()
         start_load(0)
+
+    @pl.when(stage < 3)
+    def _():
+        flip_weight()
+        flip_normed()
 
     def body(i, carry):
         @pl.when(i < n)
@@ -452,6 +525,10 @@
         def _():
             for load in loads:
                 load.wait()
+
+            @pl.when(stage == 3)
+            def _():
+                load_out.wait()
 
         @pl.when((i >= 1) & (i <= n))
         def _():
@@ -472,7 +549,7 @@
             for j in range(hid // COLS):
                 part = pl.ds(j * COLS, COLS)
                 gate_pre, in_pre, gate_sig, gate_act = swiglu_parts(normed, w_gate[:, part], w_in[:, part])
-                d_hidden = lax.dot_general(both, w_out[part, :], CONTRACT_COLS, preferred_element_type=jnp.float32).astype(jnp.bfloat16).astype(jnp.float32)
+                d_hidden = jnp.dot(both, w_out[:, part], preferred_element_type=jnp.float32).astype(jnp.bfloat16).astype(jnp.float32)
                 u_out[w, :, part] = (gate_act * in_pre).astype(jnp.bfloat16)
                 d_gate = (d_hidden * in_pre * (gate_sig * (1.0 + gate_pre * (1.0 - gate_sig)))).astype(jnp.bfloat16)
                 d_up = (d_hidden * gate_act).astype(jnp.bfloat16)
@@ -544,6 +621,10 @@
         def _():
             dx_done(c)
 
+    @pl.when(stage == 3)
+    def _():
+        flip_normed()
+
     @pl.when((stage > 0) | (core > 0))
     def _():
         remote(dx_ref, dx_ref, dx_send.at[0, 0], dx_recv.at[0], peer).wait_recv()
@@ -555,8 +636,8 @@
             far_copy(c).wait_send()
 
 
-def common_scratch(width, hid, rows):
-    return [pltpu.VMEM((width, hid), jnp.bfloat16), pltpu.VMEM((width, hid), jnp.bfloat16), pltpu.VMEM((hid, width), jnp.bfloat16),
+def common_scratch(width, hid, rows, flipped):
+    return [pltpu.VMEM((width, hid), jnp.bfloat16), pltpu.VMEM((width, hid), jnp.bfloat16), pltpu.VMEM((width, hid) if flipped else (hid, width), jnp.bfloat16),
             pltpu.VMEM((DEPTH, rows, width), jnp.bfloat16)]
 
 
@@ -571,16 +652,16 @@
 def forward_phase(x_chunks, blocks):
     n, rows, width = x_chunks.shape
     half, hid = blocks[0].shape
-    whole = [jax.ShapeDtypeStruct((width, hid), jnp.bfloat16)] * 2 + [jax.ShapeDtypeStruct((hid, width), jnp.bfloat16)]
+    whole = [jax.ShapeDtypeStruct((width, hid), jnp.bfloat16)] * 2 + [jax.ShapeDtypeStruct((hid, width), jnp.bfloat16), jax.ShapeDtypeStruct((width, hid), jnp.bfloat16)]
     anywhere = pl.BlockSpec(memory_space=pl.ANY)
     return pl.pallas_call(
         forward_kernel,
         in_specs=[anywhere] * 4,
-        out_specs=[anywhere] * 6,
+        out_specs=[anywhere] * 7,
         out_shape=[jax.ShapeDtypeStruct((n, rows, width), jnp.bfloat16), jax.ShapeDtypeStruct((n, 2 * rows, width), jnp.bfloat16), jax.ShapeDtypeStruct((n, rows, width), jnp.bfloat16)] + whole,
-        scratch_shapes=common_scratch(width, hid, rows) + [pltpu.VMEM((4, rows, width), jnp.bfloat16)] * 2 + partial_scratch(width, rows)
-        + dma(6, 2, 2, DEPTH, 4, 4, 3, 3, DEPTH, 4, 4, n, n)
-        + [pltpu.VMEM((3, half, hid // RELAYED), jnp.bfloat16), pltpu.SemaphoreType.DMA((4, 3)), pltpu.SemaphoreType.DMA((4, 3))] + [pltpu.SemaphoreType.REGULAR],
+        scratch_shapes=common_scratch(width, hid, rows, False) + [pltpu.VMEM((4, rows, width), jnp.bfloat16)] * 2 + partial_scratch(width, rows)
+        + dma(7, 2, 2, DEPTH, 4, 4, 3, 3, DEPTH, 4, 4, n, n)
+        + [pltpu.VMEM((3, half, hid // RELAYED), jnp.bfloat16), pltpu.VMEM((width, hid), jnp.bfloat16), pltpu.SemaphoreType.DMA((4, 3)), pltpu.SemaphoreType.DMA((4, 3))] + [pltpu.SemaphoreType.REGULAR],
         cost_estimate=pl.CostEstimate(flops=12 * n * rows * width * hid, bytes_accessed=6 * width * hid, transcendentals=0),
         compiler_params=pltpu.CompilerParams(has_side_effects=True, vmem_limit_bytes=VMEM_BYTES),
         name="forward_phase",
@@ -594,13 +675,15 @@
     wide = jax.ShapeDtypeStruct((n, 2 * rows, hid), jnp.bfloat16)
     return pl.pallas_call(
         backward_kernel,
-        in_specs=[anywhere] * 6,
-        out_specs=[anywhere] * 6,
-        out_shape=[jax.ShapeDtypeStruct((n, rows, width), jnp.bfloat16), jax.ShapeDtypeStruct((n, 2 * rows, width), jnp.bfloat16), wide, wide, wide, jax.ShapeDtypeStruct((n, rows, width), jnp.bfloat16)],
-        scratch_shapes=common_scratch(width, hid, rows)
+        in_specs=[anywhere] * 7,
+        out_specs=[anywhere] * 7,
+        out_shape=[jax.ShapeDtypeStruct((n, rows, width), jnp.bfloat16), jax.ShapeDtypeStruct((n, 2 * rows, width), jnp.bfloat16), wide, wide, wide, jax.ShapeDtypeStruct((n, rows, width), jnp.bfloat16), jax.ShapeDtypeStruct((width, n * 2 * rows), jnp.bfloat16)],
+        scratch_shapes=common_scratch(width, hid, rows, True)
         + [pltpu.VMEM((3, rows, width), jnp.bfloat16), pltpu.VMEM((3, 2 * rows, width), jnp.bfloat16), pltpu.VMEM((3, rows, width), jnp.bfloat16)]
         + partial_scratch(width, rows) + [pltpu.VMEM((2, 2 * rows, hid), jnp.bfloat16)] * 3
-        + dma(3, 2, 3, 3, 2, DEPTH, 3, 3, 3, 3, 3, 3, 2, 2, 2, 2) + [pltpu.SemaphoreType.DMA((2, 4))] + dma(1, n, n) + [pltpu.SemaphoreType.REGULAR],
+        + dma(3, 2, 3, 3, 2, DEPTH, 3, 3, 3, 3, 3, 3, 2, 2, 2, 2) + [pltpu.SemaphoreType.DMA((2, 4))] + dma(1, n, n)
+        + [pltpu.VMEM((2, COLS, width), jnp.bfloat16), pltpu.VMEM((2, COLS // (2 * rows), 2 * rows, width), jnp.bfloat16), pltpu.VMEM((2, width, COLS), jnp.bfloat16)]
+        + dma(2, 2) + [pltpu.SemaphoreType.REGULAR],
         cost_estimate=pl.CostEstimate(flops=20 * n * rows * width * hid, bytes_accessed=6 * width * hid, transcendentals=0),
         compiler_params=pltpu.CompilerParams(has_side_effects=True, vmem_limit_bytes=VMEM_BYTES),
         name="backward_phase",
@@ -611,7 +694,7 @@
                     raw, flipped, tile, mine, give, got, total, total_t,
                     raw_sem, tile_sem, p_send, p_recv, keep_sem, keep_t_sem, far_send, far_t_send, far_recv):
     z, y, x, core = (lax.axis_index(name) for name in ALL_AXES)
-    tokens, width = n_ref.shape
+    tokens, width = e_ref.shape
     hid = da_ref.shape[1]
     half = width // 2
     tiles = hid // COLS
@@ -668,10 +751,13 @@
 
             flipped[:, cols(k)] = raw[lax.rem(k, 2)].T
 
+    whole_load = pltpu.make_async_copy(n_ref, flipped, raw_sem.at[0])
+    whole_load.start()
     tile_load(0, 0).start()
+    whole_load.wait()
     for a in range(3):
-        if a != 1:
-            flip(n_ref if a == 0 else e_ref)
+        if a == 2:
+            flip(e_ref)
 
         @pl.loop(0, tiles)
         def _(j, a=a):
@@ -743,7 +829,7 @@
 
 
 def gradients(n_flat, e_flat, da_flat, db_flat, u_flat):
-    tokens, width = n_flat.shape
+    tokens, width = e_flat.shape
     hid = da_flat.shape[1]
     half = width // 2
     anywhere = pl.BlockSpec(memory_space=pl.ANY)
@@ -775,12 +861,12 @@
         n_chunks = x_in_chunks.shape[0]
 
         saved_h, saved_n, _, *weights = forward_phase(x_in_chunks, [w[0, 0] for w in (w_gate, w_in, w_out)])
-        dx, saved_e, saved_u, saved_da, saved_db, _ = backward_phase(g_in_chunks, saved_h, saved_n, weights)
+        dx, saved_e, saved_u, saved_da, saved_db, _, n_t = backward_phase(g_in_chunks, saved_h, saved_n, weights)
 
         def flat(array):
             return array.reshape(n_chunks * 2 * ROWS, array.shape[-1])
 
-        grads = gradients(flat(saved_n), flat(saved_e), flat(saved_da), flat(saved_db), flat(saved_u))
+        grads = gradients(n_t, flat(saved_e), flat(saved_da), flat(saved_db), flat(saved_u))
         dw_gate, dw_in, dw_out = (grad[None, None] for grad in grads)
         return dx.reshape(x_in.shape), dw_gate, dw_in, dw_out
 

time: 1350 us -> 1330 us (0.985)
  Pallas kernels: 1320 us -> 1300 us
    pallas_call x1, Pallas kernels: 555 us -> 540 us  [backward_phase(): pl.pallas_call(backward_kernel, in_specs=[anywhere] * 7, out_specs=[anywh...]
where the time goes in v1:
time: 1330 us
  Pallas kernels  1300 us (98%)
  local copies, waits for them, and re-layouts  24.6 us (2%)
    pallas_call x1, Pallas kernels, backward_phase(): pl.pallas_call(backward_kernel, in_specs=[anywhere] * 7, out_specs=[anywh...  540 us
    pallas_call x1, Pallas kernels, forward_phase(): pl.pallas_call(forward_kernel, in_specs=[anywhere] * 4, out_specs=[anywhe...  436 us
    pallas_call x1, Pallas kernels, gradients(): pl.pallas_call(gradient_kernel, in_specs=[anywhere] * 5, out_specs=[anywh...  325 us

profile of v1, /device:TPU:1, one launch (start us, length us, event | category | flops | bytes accessed | tf_op | source)
XLA Modules:
  0.0 1326.0 jit_solution(854823386253581388)
XLA Ops:
  0.6 435.9 %forward_phase.1 = (bf16[24,64,1536]{2,1,0:T(8,128)(2,1)}, bf16[24,128,1536]{2,1,0:T(8,128)(2,1)}, bf16[24,64,1536]{2,1,0:T(8,128)(2,1)}, bf16[1536,3072]{1,0:T(...) custom-call(bf16[24,64,1536]{2,1,0:T(8,128)(2,1)} %bitcast.19, ...), custom_call_target="tpu_custom_call" | custom-call | flops 86973087744 | bytes 28311552 | tf_op jit(solution)/shard_map/forward_phase/pallas_call | solution.py:657
  436.5 539.5 %backward_phase.1 = (bf16[24,64,1536]{2,1,0:T(8,128)(2,1)}, bf16[24,128,1536]{2,1,0:T(8,128)(2,1)}, bf16[24,128,3072]{2,1,0:T(8,128)(2,1)}, bf16[24,128,3072]{2,...) custom-call(bf16[24,64,1536]{2,1,0:T(8,128)(2,1)} %bitcast.23, ...), custom_call_target="tpu_custom_call" | custom-call | flops 144955146240 | bytes 28311552 | tf_op jit(solution)/shard_map/backward_phase/pallas_call | solution.py:676
  976.1 325.3 %gradients.1 = (f32[768,3072]{1,0:T(8,128)}, f32[768,3072]{1,0:T(8,128)}, f32[3072,768]{1,0:T(8,128)}) custom-call(bf16[1536,3072]{1,0:T(8,128)(2,1)} %get-tuple-element.26.n_ref, bf16[3072,1536]{1,0:T(8,128)(2,1)} %bitcast.27, bf16[3072,3072]{1,0:T(8,128)(2,1)} %bitcast.25, bf16[3072,3072]{1,0:T(8,128)(2,1)} %bitcast.26, bf16[3072,3072]{1,0:T(8,128)(2,1)} %bitcast.24), custom_call_target="tpu_custom_call" | custom-call | flops 86973087744 | bytes 56623104 | tf_op jit(solution)/shard_map/gradients/pallas_call | solution.py:836
  1301.4 4.8 copy.13
  1306.2 0.0 copy-start
  1306.2 0.0 slice-start
  1306.2 0.0 slice-start.1
  1306.2 9.8 copy.14
  1316.0 0.0 copy-done
  1316.0 0.0 slice-start.2
  1316.0 4.8 copy.15
  1320.8 0.0 slice-done
  1320.8 0.9 slice-done.1
  1321.7 0.5 slice-done.2
  1322.2 3.7 copy.16
  (1 shorter events, 0.0 us)
Async XLA Ops:
  1306.2 9.8 copy-start
  1306.2 14.6 %slice-start = ((s8[9437184]{0:T(1024)(128)(4,1)}), s8[4194304]{0:T(1024)(128)(4,1)S(1)}, s32[]{:S(2)}) async-start(s8[9437184]{0:T(1024)(128)(4,1)} %bitcast.13), calls=%async_computation | async-start | bytes 8388608
  1306.2 15.5 %slice-start.1 = ((s8[9437184]{0:T(1024)(128)(4,1)}), s8[4194304]{0:T(1024)(128)(4,1)S(1)}, s32[]{:S(2)}) async-start(s8[9437184]{0:T(1024)(128)(4,1)} %bitcast.13), calls=%async_computation.1 | async-start | bytes 8388608
  1316.0 6.2 slice-start.2
